TPU v7x, 32 devices: a whole 2x2x4 slice. The times are simulated.
32 devices in a mesh: grp: 4 (over y, x), dev: 8 (over z, core).
Axes of the slice: x: 2, y: 2, z: 4, core: 2. Of those that a mesh axis runs over, the one named last changes fastest.
Arguments:
- source_id: int32 [524288], P(('grp', 'dev')), may hold values from 0 to 4095, as said below
- slot: int32 [524288], P(('grp', 'dev')), may hold values from 0 to 127, as said below
- owner: int32 [4096], replicated, may hold values from 0 to 4095, as said below
- counts: int32 [4096], P(('grp', 'dev')), may hold values from 1 to 128, as said below
- partials: float32 [5, 524288], P(None, ('grp', 'dev')), may hold values from -6 to 6
- residual: float32 [524288], P(('grp', 'dev')), may hold values from -6 to 6
- weight: float32 [524288], P(('grp', 'dev')), may hold values from 0.3 to 9
- prior: float32 [5, 4096], P(None, ('grp', 'dev')), may hold values from 0.5 to 4
Outputs:
- updates: float32 [5, 4096], P(None, ('grp', 'dev'))
- standardized: float32 [524288], P(('grp', 'dev'))
- norm: float32 [], replicated
Inputs may be any that keep to these rules, and one draw needn't show every extreme that they name: A permutation: source s stands at owner position owner[s], and position p belongs to device p // 128. `source_id`: the rows of one device stand in 32 aligned blocks of 512 rows; block k holds only rows whose source's owner position lies in device k's range. Over all rows, each pair of a source and a slot below 128 appears exactly once. A row is an observation when its slot is below its source's count, else padding. Each device's block of counts holds 128 at least once.
All inputs are finite; a program needn't handle non-finite values.
Results may differ from a plain program's by a relative error of at most 0.0003.
Values sent between devices are 32-bit elements; how exact they have to be, the bound alone decides.
A program may use at most 64 MiB of HBM per device.

v0:
```python
import jax
import jax.numpy as jnp
from jax import lax
from jax.sharding import PartitionSpec as P


def solve_blocks(normal, moments):
    params = len(moments)
    factor = {}
    for column in range(params):
        running = normal[column][column]
        for earlier in range(column):
            running = running - factor[column, earlier] ** 2
        pivot_value = jnp.sqrt(running)
        factor[column, column] = pivot_value
        for target in range(column + 1, params):
            current = normal[target][column]
            for earlier in range(column):
                current = current - factor[target, earlier] * factor[column, earlier]
            factor[target, column] = current / pivot_value
    forward = []
    for target in range(params):
        current = moments[target]
        for earlier in range(target):
            current = current - factor[target, earlier] * forward[earlier]
        forward.append(current / factor[target, target])
    backward = [None] * params
    for target in reversed(range(params)):
        current = forward[target]
        for later in range(target + 1, params):
            current = current - factor[later, target] * backward[later]
        backward[target] = current / factor[target, target]
    return jnp.stack(backward)


def spread_rows(table, onehot):
    return lax.dot_general(table, onehot, (((1,), (1,)), ((), ())), precision=lax.Precision.HIGHEST)


def body(source_id, slot, owner, counts, partials, residual, weight, prior):
    group_count = lax.axis_size("grp")
    member_count = lax.axis_size("dev")
    params = partials.shape[0]
    fields_count = params + 2
    row_count = residual.shape[0]
    src_local = counts.shape[0]
    pad_slots = row_count // src_local
    block_rows = row_count // (group_count * member_count)
    position = owner[source_id]
    cell_index = position % src_local * pad_slots + slot
    fields = jnp.concatenate([partials, residual[None, :], weight[None, :]], axis=0)
    outgoing = (
        fields.reshape(fields_count, group_count, member_count, block_rows),
        cell_index.reshape(1, group_count, member_count, block_rows),
    )
    arrived, arrived_cell = (
        lax.all_to_all(
            lax.all_to_all(outgoing[0], "dev", split_axis=2, concat_axis=2, tiled=True),
            "grp",
            split_axis=1,
            concat_axis=1,
            tiled=True,
        ),
        lax.all_to_all(
            lax.all_to_all(outgoing[1], "dev", split_axis=2, concat_axis=2, tiled=True),
            "grp",
            split_axis=1,
            concat_axis=1,
            tiled=True,
        ),
    )
    arrived = arrived.reshape(fields_count, row_count)
    arrived_cell = arrived_cell.reshape(row_count)
    count_table = counts.astype(jnp.float32)[None, :]
    step_rows = min(row_count, 4096)
    step_count = row_count // step_rows
    columns = jnp.arange(src_local, dtype=jnp.int32)[None, :]
    pairs = [
        (first_idx, second_idx)
        for first_idx in range(params)
        for second_idx in range(first_idx, params)
    ]

    def block_view(index):
        start = index * step_rows
        piece = lax.dynamic_slice_in_dim(arrived, start, step_rows, 1)
        cells = lax.dynamic_slice_in_dim(arrived_cell, start, step_rows, 0)
        onehot = ((cells // pad_slots)[:, None] == columns).astype(jnp.float32)
        row_counts = spread_rows(count_table, onehot)[0]
        live = ((cells % pad_slots).astype(jnp.float32) < row_counts).astype(jnp.float32)
        return (piece, onehot, live)

    def accumulate(index, total):
        piece, onehot, live = block_view(index)
        slopes = piece[0:params]
        observed = piece[params]
        weighted = slopes * (piece[params + 1] * live)[None]
        terms = [weighted[first_idx] * slopes[second_idx] for first_idx, second_idx in pairs]
        terms = terms + [weighted[first_idx] * observed for first_idx in range(params)]
        stats = jnp.stack(terms)
        return total + jnp.dot(stats, onehot, precision=lax.Precision.HIGHEST)

    sums = lax.fori_loop(
        0, step_count, accumulate, jnp.zeros((len(pairs) + params, src_local), jnp.float32)
    )
    normal = [[None] * params for _ in range(params)]
    for pair_idx, (first_idx, second_idx) in enumerate(pairs):
        entry = sums[pair_idx]
        if first_idx == second_idx:
            entry = entry + prior[first_idx]
        normal[first_idx][second_idx] = entry
        normal[second_idx][first_idx] = entry
    moments = [sums[len(pairs) + first_idx] for first_idx in range(params)]
    updates = solve_blocks(normal, moments)

    def refit(index, fresh_rows):
        piece, onehot, live = block_view(index)
        fitted = jnp.sum(piece[0:params] * spread_rows(updates, onehot), axis=0)
        fresh_block = (piece[params] - fitted) * live
        return lax.dynamic_update_slice_in_dim(fresh_rows, fresh_block, index * step_rows, 0)

    fresh_cells = lax.fori_loop(0, step_count, refit, jnp.zeros((row_count,), jnp.float32))
    returned = lax.all_to_all(
        lax.all_to_all(
            fresh_cells.reshape(1, group_count, member_count, block_rows),
            "grp",
            split_axis=1,
            concat_axis=1,
            tiled=True,
        ),
        "dev",
        split_axis=2,
        concat_axis=2,
        tiled=True,
    )
    fresh = returned.reshape(row_count)
    totals = lax.psum(
        jnp.stack([jnp.sum(weight * fresh * fresh), jnp.sum(counts.astype(jnp.float32))]),
        ("grp", "dev"),
    )
    norm = jnp.sqrt(totals[0] / totals[1] + 1e-06)
    return (updates, fresh * jnp.sqrt(weight) / norm, norm)


def solution(mesh):
    in_specs = (
        P(("grp", "dev")),
        P(("grp", "dev")),
        P(),
        P(("grp", "dev")),
        P(None, ("grp", "dev")),
        P(("grp", "dev")),
        P(("grp", "dev")),
        P(None, ("grp", "dev")),
    )
    out_specs = (P(None, ("grp", "dev")), P(("grp", "dev")), P())
    return jax.shard_map(body, mesh=mesh, in_specs=in_specs, out_specs=out_specs, check_vma=False)
```

profile of v0, /device:TPU:0, one launch (start us, length us, event | category | flops | bytes accessed | tf_op | source)
XLA Modules:
  0.0 230.4 jit_solution(10447145855971860731)
XLA Ops:
  1.5 90.5 %gather_fusion = s32[16384]{0:T(1024)S(1)} fusion(s32[4096]{0:T(1024)S(1)} %copy-done, s32[16384]{0:T(1024)S(1)} %fusion.29), kind=kCustom, calls=%fused_computation | custom fusion | bytes 196608 | tf_op jit(solution)/shard_map/gather | solution.py:49
  92.8 6.5 %all-to-all-start.2 = ((s32[1,4,8,512]{3,1,0,2:T(4,128)}), s32[1,4,8,512]{3,1,0,2:T(4,128)S(1)}, u32[]{:S(2)}, u32[]{:S(2)}) async-start(s32[1,4,8,512]{3,1,0,2:T(4,128)} %copy.17), calls=%async_computation.2 | async-start | bytes 131072 | tf_op jit(solution)/shard_map/all_to_all | solution.py:65
  101.3 3.9 %all-to-all-done.2 = s32[1,4,8,512]{3,1,0,2:T(4,128)S(1)} async-done(((s32[1,4,8,512]{3,1,0,2:T(4,128)}), s32[1,4,8,512]{3,1,0,2:T(4,128)S(1)}, u32[]{:S(2)}, u32[]{:S(2)}) %all-to-all-start.2) | async-done | bytes 65568 | tf_op jit(solution)/shard_map/all_to_all | solution.py:65
  105.2 3.5 %all-to-all-start = ((f32[7,4,8,512]{3,1,0,2:T(4,128)}), f32[7,4,8,512]{3,1,0,2:T(4,128)S(1)}, u32[]{:S(2)}, u32[]{:S(2)}) async-start(f32[7,4,8,512]{3,1,0,2:T(4,128)} %copy.14), calls=%async_computation | async-start | bytes 917504 | tf_op jit(solution)/shard_map/all_to_all | solution.py:58
  109.4 13.2 %all-to-all-done = f32[7,4,8,512]{3,1,0,2:T(4,128)S(1)} async-done(((f32[7,4,8,512]{3,1,0,2:T(4,128)}), f32[7,4,8,512]{3,1,0,2:T(4,128)S(1)}, u32[]{:S(2)}, u32[]{:S(2)}) %all-to-all-start) | async-done | bytes 458784 | tf_op jit(solution)/shard_map/all_to_all | solution.py:58
  122.6 3.7 %all-to-all-start.3 = ((s32[1,4,8,512]{3,2,0,1:T(8,128)}), s32[1,4,8,512]{3,2,0,1:T(8,128)S(1)}, u32[]{:S(2)}, u32[]{:S(2)}) async-start(s32[1,4,8,512]{3,2,0,1:T(8,128)} %copy.18), calls=%async_computation.3 | async-start | bytes 131072 | tf_op jit(solution)/shard_map/all_to_all | solution.py:64
  127.2 3.9 %all-to-all-done.3 = s32[1,4,8,512]{3,2,0,1:T(8,128)S(1)} async-done(((s32[1,4,8,512]{3,2,0,1:T(8,128)}), s32[1,4,8,512]{3,2,0,1:T(8,128)S(1)}, u32[]{:S(2)}, u32[]{:S(2)}) %all-to-all-start.3) | async-done | bytes 65568 | tf_op jit(solution)/shard_map/all_to_all | solution.py:64
  131.1 3.5 %all-to-all-start.1 = ((f32[7,4,8,512]{3,2,0,1:T(8,128)}), f32[7,4,8,512]{3,2,0,1:T(8,128)S(1)}, u32[]{:S(2)}, u32[]{:S(2)}) async-start(f32[7,4,8,512]{3,2,0,1:T(8,128)} %copy.15), calls=%async_computation.1 | async-start | bytes 917504 | tf_op jit(solution)/shard_map/all_to_all | solution.py:57
  134.7 6.1 %all-to-all-done.1 = f32[7,4,8,512]{3,2,0,1:T(8,128)S(1)} async-done(((f32[7,4,8,512]{3,2,0,1:T(8,128)}), f32[7,4,8,512]{3,2,0,1:T(8,128)S(1)}, u32[]{:S(2)}, u32[]{:S(2)}) %all-to-all-start.1) | async-done | bytes 458784 | tf_op jit(solution)/shard_map/all_to_all | solution.py:57
  141.1 14.9 %while.33 = (s32[]{:T(128)}, f32[20,128]{1,0:T(8,128)S(1)}, f32[7,16384]{1,0:T(8,128)S(1)}, s32[16384]{0:T(1024)S(1)}, f32[1,128]{1,0:T(1,128)S(1)}, /*index=5*/...) while((s32[]{:T(128)}, f32[20,128]{1,0:T(8,128)S(1)}, ...), condition=%wide.region_1.2_spmd.clone, body=%wide.region_0.1_spmd.clone.sunk | while | flops 133391376 | bytes 2028365 | solution.py:103
  148.6 1.5 fusion.48
  152.4 1.5 fusion.48
  156.2 12.7 %while.32 = (s32[]{:T(128)}, f32[16384]{0:T(1024)S(1)}, s32[16384]{0:T(1024)S(1)}, f32[1,128]{1,0:T(1,128)S(1)}, f32[7,16384]{1,0:T(8,128)S(1)}, /*index=5*/f32[...) while((s32[]{:T(128)}, f32[16384]{0:T(1024)S(1)}, ...), condition=%wide.region_4.5_spmd.clone, body=%wide.region_2.4_spmd.clone.sunk | while | flops 38952968 | bytes 306359 | solution.py:122
  156.3 1.5 fusion.44
  157.8 1.5 fusion.45
  159.5 1.5 fusion.44
  161.0 1.5 fusion.45
  162.6 1.5 fusion.44
  164.1 1.5 fusion.45
  165.8 1.5 fusion.44
  169.0 7.4 %all_to_all.30 = f32[1,4,8,512]{3,2,0,1:T(8,128)S(1)} all-to-all(f32[1,4,8,512]{3,2,0,1:T(8,128)S(1)} %reshape.57), channel_id=1, replica_groups=mesh['grp'=4,'dev'=8] {'grp'}, dimensions={1} | all-to-all | bytes 131072 | tf_op jit(solution)/shard_map/all_to_all | solution.py:124
  177.1 3.4 %all-to-all-start.5 = ((f32[1,4,8,512]{3,1,0,2:T(4,128)}), f32[1,4,8,512]{3,1,0,2:T(4,128)S(1)}, u32[]{:S(2)}, u32[]{:S(2)}) async-start(f32[1,4,8,512]{3,1,0,2:T(4,128)} %copy.19), calls=%async_computation.5 | async-start | bytes 131072 | tf_op jit(solution)/shard_map/all_to_all | solution.py:123
  181.0 5.2 %all-to-all-done.5 = f32[1,4,8,512]{3,1,0,2:T(4,128)S(1)} async-done(((f32[1,4,8,512]{3,1,0,2:T(4,128)}), f32[1,4,8,512]{3,1,0,2:T(4,128)S(1)}, u32[]{:S(2)}, u32[]{:S(2)}) %all-to-all-start.5) | async-done | bytes 65568 | tf_op jit(solution)/shard_map/all_to_all | solution.py:123
  188.3 38.4 %psum.7 = f32[2]{0:T(128)S(1)} all-reduce(f32[2]{0:T(128)S(1)} %pad_maximum_fusion.1), channel_id=1, replica_groups=mesh['grp'=4,'dev'=8] {'grp','dev'}, use_global_device_ids=true, to_apply=%region_7.8 | all-reduce | flops 2 | bytes 16 | tf_op jit(solution)/shard_map/psum | solution.py:137
  (93 shorter events, 23.9 us)
Async XLA Ops:
  0.6 0.9 copy-start
  1.5 90.6 %copy-start.3 = (s32[16384]{0:T(1024)S(1)}, s32[16384]{0:T(1024)}, u32[]{:S(2)}) copy-start(s32[16384]{0:T(1024)} %param.13) | copy-start | bytes 196612
  92.1 7.2 %copy-start.2 = (f32[5,16384]{1,0:T(8,128)S(1)}, f32[5,16384]{1,0:T(8,128)}, u32[]{:S(2)}) copy-start(f32[5,16384]{1,0:T(8,128)} %param.16) | copy-start | bytes 983044
  92.8 6.7 %copy-start.4 = (f32[16384]{0:T(1024)S(1)}, f32[16384]{0:T(1024)}, u32[]{:S(2)}) copy-start(f32[16384]{0:T(1024)} %param.17) | copy-start | bytes 196612
  92.8 12.4 %all-to-all-start.2 = ((s32[1,4,8,512]{3,1,0,2:T(4,128)}), s32[1,4,8,512]{3,1,0,2:T(4,128)S(1)}, u32[]{:S(2)}, u32[]{:S(2)}) async-start(s32[1,4,8,512]{3,1,0,2:T(4,128)} %copy.17), calls=%async_computation.2 | async-start | bytes 131072 | tf_op jit(solution)/shard_map/all_to_all | solution.py:65
  99.3 0.8 copy-start.1
  105.2 17.3 %all-to-all-start = ((f32[7,4,8,512]{3,1,0,2:T(4,128)}), f32[7,4,8,512]{3,1,0,2:T(4,128)S(1)}, u32[]{:S(2)}, u32[]{:S(2)}) async-start(f32[7,4,8,512]{3,1,0,2:T(4,128)} %copy.14), calls=%async_computation | async-start | bytes 917504 | tf_op jit(solution)/shard_map/all_to_all | solution.py:58
  122.6 8.6 %all-to-all-start.3 = ((s32[1,4,8,512]{3,2,0,1:T(8,128)}), s32[1,4,8,512]{3,2,0,1:T(8,128)S(1)}, u32[]{:S(2)}, u32[]{:S(2)}) async-start(s32[1,4,8,512]{3,2,0,1:T(8,128)} %copy.18), calls=%async_computation.3 | async-start | bytes 131072 | tf_op jit(solution)/shard_map/all_to_all | solution.py:64
  127.2 7.4 %copy-start.7 = (s32[128]{0:T(128)S(1)}, s32[128]{0:T(128)}, u32[]{:S(2)}) copy-start(s32[128]{0:T(128)} %param.15) | copy-start | bytes 1540
  131.1 9.7 %all-to-all-start.1 = ((f32[7,4,8,512]{3,2,0,1:T(8,128)}), f32[7,4,8,512]{3,2,0,1:T(8,128)S(1)}, u32[]{:S(2)}, u32[]{:S(2)}) async-start(f32[7,4,8,512]{3,2,0,1:T(8,128)} %copy.15), calls=%async_computation.1 | async-start | bytes 917504 | tf_op jit(solution)/shard_map/all_to_all | solution.py:57
  141.1 14.9 %copy-start.6 = (f32[5,128]{1,0:T(8,128)S(1)}, f32[5,128]{1,0:T(8,128)}, u32[]{:S(2)}) copy-start(f32[5,128]{1,0:T(8,128)} %param.19) | copy-start | bytes 7684
  169.0 60.4 %copy-start.5 = (f32[5,128]{1,0:T(8,128)}, f32[5,128]{1,0:T(8,128)S(1)}, u32[]{:S(2)}) copy-start(f32[5,128]{1,0:T(8,128)S(1)} %get-tuple-element.647) | copy-start | bytes 7684
  177.1 9.2 %all-to-all-start.5 = ((f32[1,4,8,512]{3,1,0,2:T(4,128)}), f32[1,4,8,512]{3,1,0,2:T(4,128)S(1)}, u32[]{:S(2)}, u32[]{:S(2)}) async-start(f32[1,4,8,512]{3,1,0,2:T(4,128)} %copy.19), calls=%async_computation.5 | async-start | bytes 131072 | tf_op jit(solution)/shard_map/all_to_all | solution.py:123
where the time goes:
time: 231 us; the launch traced here: 230 us
  local copies, waits for them, and re-layouts  99.3 us (43%)
  blocking collectives  45.8 us (20%)
  waiting for transfers between devices  32.4 us (14%)
  matrix products  21.7 us (9%)
  starting transfers between devices  20.5 us (9%)
  other arithmetic  6.75 us (3%)
  between operations  3.41 us (1%)
    gather x1, local copies, waits for them, and re-layouts, body(): position = owner[source_id]  90.5 us
    psum x1, blocking collectives, body(): lax.psum(jnp.stack([jnp.sum(weight * fresh * fresh), jnp.sum(counts.astyp...  38.4 us
    dot_general x12, matrix products, spread_rows(): lax.dot_general(table, onehot, (((1,), (1,)), ((), ())), precision=lax.Pr...  17.7 us
    all_to_all x1, waiting for transfers between devices, body(): lax.all_to_all(outgoing[0], 'dev', split_axis=2, concat_axis=2, tiled=True)  13.2 us
    all_to_all x1, blocking collectives, body(): lax.all_to_all(fresh_cells.reshape(1, group_count, member_count, block_ro...  7.43 us
    all_to_all x1, starting transfers between devices, body(): lax.all_to_all(outgoing[1], 'dev', split_axis=2, concat_axis=2, tiled=True)  6.49 us
    all_to_all x1, waiting for transfers between devices, body(): lax.all_to_all(lax.all_to_all(outgoing[0], 'dev', split_axis=2, concat_ax...  6.14 us
    all_to_all x1, waiting for transfers between devices, body(): lax.all_to_all(lax.all_to_all(fresh_cells.reshape(1, group_count, member_...  5.25 us
  transfers between devices with their start and end apart: 5, of which 5 were waited for; matrix products, arithmetic and copies ran while one was open for 2% of the time, Pallas kernels for 0%

commit v1 on v0

v1 whole, which is shorter than its diff:
```python
import functools

import jax
import jax.numpy as jnp
from jax import lax
from jax.experimental import pallas as pl
from jax.experimental.pallas import tpu as pltpu
from jax.sharding import PartitionSpec as P

LANES = 128
SUBLANES = 8
MESH = pl.DeviceIdType.MESH


def solve_rows(normal, moments):
    params = len(moments)
    factor = {}
    for column in range(params):
        running = normal[column][column]
        for earlier in range(column):
            running = running - factor[column, earlier] ** 2
        pivot_value = jnp.sqrt(running)
        factor[column, column] = pivot_value
        for target in range(column + 1, params):
            current = normal[target][column]
            for earlier in range(column):
                current = current - factor[target, earlier] * factor[column, earlier]
            factor[target, column] = current / pivot_value
    forward = []
    for target in range(params):
        current = moments[target]
        for earlier in range(target):
            current = current - factor[target, earlier] * forward[earlier]
        forward.append(current / factor[target, target])
    backward = [None] * params
    for target in reversed(range(params)):
        current = forward[target]
        for later in range(target + 1, params):
            current = current - factor[later, target] * backward[later]
        backward[target] = current / factor[target, target]
    return backward


def thirds(values):
    high = values.astype(jnp.bfloat16).astype(jnp.float32)
    rest = values - high
    middle = rest.astype(jnp.bfloat16).astype(jnp.float32)
    return [high, middle, rest - middle]


def stacked(values, rows):
    terms = thirds(values)
    spare = rows - 3 * values.shape[0]
    if spare:
        terms.append(jnp.zeros((spare, values.shape[1]), jnp.float32))
    return jnp.concatenate(terms, axis=0).astype(jnp.bfloat16)


def kernel(
    sizes,
    source_ref, slot_ref, owner_ref, counts_ref, partials_ref, residual_ref, weight_ref, prior_ref,
    updates_ref, fresh_ref, norm_ref,
    out_buf, in_buf, hot_buf, back_out, back_in,
    send_sem, recv_sem, back_send_sem, back_recv_sem,
):
    n, members, width = sizes
    params = partials_ref.shape[0]
    src_local = counts_ref.shape[1]
    me = lax.axis_index("grp") * members + lax.axis_index("dev")

    def coords(device):
        return (device // members, device % members)

    barrier = pltpu.get_barrier_semaphore()

    def greet(step, carry):
        peer = (me + step) % n
        pl.semaphore_signal(barrier, inc=1, device_id=coords(peer), device_id_type=MESH)
        return carry

    lax.fori_loop(1, n, greet, 0)

    def prepare(k, carry):
        cols = pl.ds(pl.multiple_of(k * width, LANES), width)
        root = jnp.sqrt(weight_ref[:, cols])
        out_buf[k, 0:params, :] = partials_ref[:, cols] * root
        out_buf[k, params : params + 1, :] = residual_ref[:, cols] * root
        out_buf[k, params + 1 : params + 2, :] = source_ref[:, cols].astype(jnp.float32)
        out_buf[k, params + 2 : params + 3, :] = slot_ref[:, cols].astype(jnp.float32)
        return carry

    lax.fori_loop(0, n, prepare, 0)

    pl.semaphore_wait(barrier, n - 1)

    def send(step, carry):
        peer = (me + step) % n
        pltpu.make_async_remote_copy(
            src_ref=out_buf.at[peer],
            dst_ref=in_buf.at[me],
            send_sem=send_sem,
            recv_sem=recv_sem.at[me],
            device_id=coords(peer),
            device_id_type=MESH,
        ).start()
        return carry

    lax.fori_loop(1, n, send, 0)

    position = me * src_local + lax.broadcasted_iota(jnp.int32, (src_local, LANES), 0)

    def invert(tile, total):
        ids = tile * LANES + lax.broadcasted_iota(jnp.int32, (1, LANES), 1)
        return total + jnp.where(owner_ref[pl.ds(tile, 1), :] == position, ids, 0)

    found = lax.fori_loop(0, owner_ref.shape[0], invert, jnp.zeros((src_local, LANES), jnp.int32))
    source_at = jnp.sum(found.astype(jnp.float32), axis=1, keepdims=True)

    counts = counts_ref[...].astype(jnp.float32)
    count_table = jnp.broadcast_to(counts, (2 * SUBLANES, src_local)).astype(jnp.bfloat16)

    def absorb(k, total):
        rows = in_buf[k]
        hot = (rows[params + 1 : params + 2, :] == source_at).astype(jnp.float32).astype(jnp.bfloat16)
        hot_buf[k] = hot
        row_counts = jnp.dot(count_table, hot, preferred_element_type=jnp.float32)[0:SUBLANES]
        rows = jnp.where(rows[params + 2 : params + 3, :] < row_counts, rows, 0.0)
        in_buf[k] = rows
        products = jnp.concatenate([rows[i : i + 1, :] * rows for i in range(params)], axis=0)
        return total + lax.dot_general(
            stacked(products, LANES), hot, (((1,), (1,)), ((), ())), preferred_element_type=jnp.float32
        )

    in_buf[me] = out_buf[me]
    total = absorb(me, jnp.zeros((LANES, src_local), jnp.float32))

    def arrive(step, total):
        peer = (me + n - step) % n
        pltpu.make_async_remote_copy(
            src_ref=out_buf.at[peer],
            dst_ref=in_buf.at[peer],
            send_sem=send_sem,
            recv_sem=recv_sem.at[peer],
            device_id=coords(peer),
            device_id_type=MESH,
        ).wait_recv()
        return absorb(peer, total)

    total = lax.fori_loop(1, n, arrive, total)

    height = params * SUBLANES
    sums = total[0:height] + total[height : 2 * height] + total[2 * height : 3 * height]
    normal = [[None] * params for _ in range(params)]
    for i in range(params):
        for j in range(i, params):
            entry = sums[i * SUBLANES + j : i * SUBLANES + j + 1]
            if i == j:
                entry = entry + prior_ref[i : i + 1, :]
            normal[i][j] = entry
            normal[j][i] = entry
    moments = [sums[i * SUBLANES + params : i * SUBLANES + params + 1] for i in range(params)]
    updates = solve_rows(normal, moments)
    for i in range(params):
        updates_ref[i : i + 1, :] = updates[i]
    blank = jnp.zeros((1, src_local), jnp.float32)
    table = jnp.concatenate(updates + [blank - 1.0, blank, blank], axis=0)
    table = stacked(table, 4 * SUBLANES)

    def refit(k, squares):
        spread = jnp.dot(table, hot_buf[k], preferred_element_type=jnp.float32)
        spread = spread[0:SUBLANES] + spread[SUBLANES : 2 * SUBLANES] + spread[2 * SUBLANES : 3 * SUBLANES]
        fresh = -jnp.sum(in_buf[k] * spread, axis=0, keepdims=True)
        back_out[k, :, 0:width] = fresh
        return squares + fresh * fresh

    squares = lax.fori_loop(0, n, refit, jnp.zeros((1, width), jnp.float32))
    lane = lax.broadcasted_iota(jnp.int32, (1, LANES), 1)
    square_sum = jnp.sum(squares, axis=1, keepdims=True)
    count_sum = jnp.sum(counts, axis=1, keepdims=True)
    tail = jnp.where(lane == 0, square_sum, jnp.where(lane == 1, count_sum, 0.0))

    def finish(k, carry):
        back_out[k, :, width : width + LANES] = tail
        return carry

    lax.fori_loop(0, n, finish, 0)
    back_in[me] = back_out[me]

    def send_back(step, carry):
        peer = (me + step) % n
        pltpu.make_async_remote_copy(
            src_ref=back_out.at[peer],
            dst_ref=back_in.at[me],
            send_sem=back_send_sem,
            recv_sem=back_recv_sem.at[me],
            device_id=coords(peer),
            device_id_type=MESH,
        ).start()
        return carry

    lax.fori_loop(1, n, send_back, 0)

    def collect(step, tails):
        peer = (me + n - step) % n
        pltpu.make_async_remote_copy(
            src_ref=back_out.at[peer],
            dst_ref=back_in.at[peer],
            send_sem=back_send_sem,
            recv_sem=back_recv_sem.at[peer],
            device_id=coords(peer),
            device_id_type=MESH,
        ).wait_recv()
        return tails

    lax.fori_loop(1, n, collect, 0)

    def gather_tails(k, tails):
        return tails + back_in[k, :, width : width + LANES]

    tails = lax.fori_loop(0, n, gather_tails, jnp.zeros((1, LANES), jnp.float32))
    square_total = jnp.sum(jnp.where(lane == 0, tails, 0.0), axis=1, keepdims=True)
    count_total = jnp.sum(jnp.where(lane == 1, tails, 0.0), axis=1, keepdims=True)
    norm = jnp.sqrt(square_total / count_total + 1e-06)
    norm_ref[...] = jnp.broadcast_to(norm, norm_ref.shape)
    scale = 1.0 / norm

    def emit(k, carry):
        cols = pl.ds(pl.multiple_of(k * width, LANES), width)
        fresh_ref[:, cols] = back_in[k, :, 0:width] * scale
        return carry

    lax.fori_loop(0, n, emit, 0)

    for buffer, semaphore in ((out_buf, send_sem), (back_out, back_send_sem)):
        sent = buffer.at[pl.ds(0, n - 1)]
        pltpu.make_async_remote_copy(
            src_ref=sent,
            dst_ref=sent,
            send_sem=semaphore,
            recv_sem=recv_sem.at[me],
            device_id=coords((me + 1) % n),
            device_id_type=MESH,
        ).wait_send()


def body(source_id, slot, owner, counts, partials, residual, weight, prior):
    members = lax.axis_size("dev")
    n = lax.axis_size("grp") * members
    params = partials.shape[0]
    row_count = residual.shape[0]
    src_local = counts.shape[0]
    block_rows = row_count // n
    width = -(-block_rows // LANES) * LANES

    def lay(array, fill):
        array = array.reshape(-1, row_count)
        if width == block_rows:
            return array
        blocks = array.reshape(-1, n, block_rows)
        blocks = jnp.pad(blocks, ((0, 0), (0, 0), (0, width - block_rows)), constant_values=fill)
        return blocks.reshape(-1, n * width)

    vmem = pl.BlockSpec(memory_space=pltpu.VMEM)
    updates, standardized, norm = pl.pallas_call(
        functools.partial(kernel, (n, members, width)),
        out_shape=(
            jax.ShapeDtypeStruct((params, src_local), jnp.float32),
            jax.ShapeDtypeStruct((1, n * width), jnp.float32),
            jax.ShapeDtypeStruct((1, LANES), jnp.float32),
        ),
        in_specs=[vmem] * 8,
        out_specs=(vmem, vmem, vmem),
        scratch_shapes=[
            pltpu.VMEM((n, SUBLANES, width), jnp.float32),
            pltpu.VMEM((n, SUBLANES, width), jnp.float32),
            pltpu.VMEM((n, src_local, width), jnp.bfloat16),
            pltpu.VMEM((n, 1, width + LANES), jnp.float32),
            pltpu.VMEM((n, 1, width + LANES), jnp.float32),
            pltpu.SemaphoreType.DMA,
            pltpu.SemaphoreType.DMA((n,)),
            pltpu.SemaphoreType.DMA,
            pltpu.SemaphoreType.DMA((n,)),
        ],
        compiler_params=pltpu.CompilerParams(
            collective_id=0, has_side_effects=True, vmem_limit_bytes=48 * 1024 * 1024
        ),
        name="exchange_fit",
    )(
        lay(source_id, -1),
        lay(slot, 0),
        owner.reshape(-1, LANES),
        counts.reshape(1, src_local),
        lay(partials, 0),
        lay(residual, 0),
        lay(weight, 1),
        prior,
    )
    standardized = standardized.reshape(n, width)[:, :block_rows] if width != block_rows else standardized
    return (updates, standardized.reshape(row_count), norm[0, 0])


def solution(mesh):
    in_specs = (
        P(("grp", "dev")),
        P(("grp", "dev")),
        P(),
        P(("grp", "dev")),
        P(None, ("grp", "dev")),
        P(("grp", "dev")),
        P(("grp", "dev")),
        P(None, ("grp", "dev")),
    )
    out_specs = (P(None, ("grp", "dev")), P(("grp", "dev")), P())
    return jax.shard_map(body, mesh=mesh, in_specs=in_specs, out_specs=out_specs, check_vma=False)
```

time: 231 us -> 43.1 us (0.19)
  local copies, waits for them, and re-layouts: 99.3 us -> 7.02 us
  blocking collectives: 45.8 us -> 0 us
  Pallas kernels: 0 us -> 33.8 us
  waiting for transfers between devices: 32.4 us -> 0 us
  matrix products: 21.7 us -> 0 us
  starting transfers between devices: 20.5 us -> 0 us
  other arithmetic: 6.75 us -> 0 us
    gather x1 -> x0, local copies, waits for them, and re-layouts: 90.5 us -> none  [body(): position = owner[source_id]]
    psum x1 -> x0, blocking collectives: 38.4 us -> none  [body(): lax.psum(jnp.stack([jnp.sum(weight * fresh * fresh), jnp.sum(counts.astyp...]
    pallas_call x0 -> x1, Pallas kernels: none -> 33.8 us  [body(): pl.pallas_call(functools.partial(kernel, (n, members, width)), out_shape=...]
    all_to_all x5 -> x0, waiting for transfers between devices: 32.4 us -> none  [the longest x1 13.2 us: body(): lax.all_to_all(outgoing[0], 'dev', split_axis=2, concat_axis=2, tiled=True)]
    dot_general x16 -> x0, matrix products: 21.7 us -> none  [the longest x12 17.7 us: spread_rows(): lax.dot_general(table, onehot, (((1,), (1,)), ((), ())), precision=lax.Pr...]
    all_to_all x5 -> x0, starting transfers between devices: 20.5 us -> none  [the longest x1 6.49 us: body(): lax.all_to_all(outgoing[1], 'dev', split_axis=2, concat_axis=2, tiled=True)]
    all_to_all x1 -> x0, blocking collectives: 7.43 us -> none  [body(): lax.all_to_all(fresh_cells.reshape(1, group_count, member_count, block_ro...]
    unnamed x20 -> x18, local copies, waits for them, and re-layouts: 1.15 us -> 7.02 us
  transfers between devices with their start and end apart: 5 -> 0, of which waited for: 5 -> 0; matrix products, arithmetic and copies ran while one was open for 2% -> 0% of each run, Pallas kernels for 0% -> 0%
where the time goes in v1:
time: 43.1 us; the launch traced here: 42.6 us
  Pallas kernels  33.8 us (78%)
  local copies, waits for them, and re-layouts  7.02 us (16%)
  between operations  1.83 us (4%)
    pallas_call x1, Pallas kernels, body(): pl.pallas_call(functools.partial(kernel, (n, members, width)), out_shape=...  33.8 us
    unnamed x18, local copies, waits for them, and re-layouts  7.02 us

profile of v1, /device:TPU:0, one launch (start us, length us, event | category | flops | bytes accessed | tf_op | source)
XLA Modules:
  0.0 42.6 jit_solution(6686260936466431555)
XLA Ops:
  0.6 0.0 copy-start.6
  0.6 0.0 copy-start.7
  0.7 0.7 %copy-done.6 = f32[5,128]{1,0:T(8,128)S(1)} copy-done((f32[5,128]{1,0:T(8,128)S(1)}, f32[5,128]{1,0:T(8,128)}, u32[]{:S(2)}) %copy-start.6) | copy-done | bytes 2584
  1.3 0.0 copy-done.7
  1.3 0.0 copy-start
  1.3 1.0 %copy-done = f32[5,16384]{1,0:T(8,128)S(1)} copy-done((f32[5,16384]{1,0:T(8,128)S(1)}, f32[5,16384]{1,0:T(8,128)}, u32[]{:S(2)}) %copy-start) | copy-done | bytes 327704
  2.4 0.0 copy-start.1
  2.4 0.8 %copy-done.1 = s32[16384]{0:T(1024)S(1)} copy-done((s32[16384]{0:T(1024)S(1)}, s32[16384]{0:T(1024)}, u32[]{:S(2)}) %copy-start.1) | copy-done | bytes 65560
  3.2 0.0 copy-start.2
  3.2 0.8 %copy-done.2 = s32[16384]{0:T(1024)S(1)} copy-done((s32[16384]{0:T(1024)S(1)}, s32[16384]{0:T(1024)}, u32[]{:S(2)}) %copy-start.2) | copy-done | bytes 65560
  4.0 0.0 copy-start.3
  4.0 0.8 %copy-done.3 = f32[16384]{0:T(1024)S(1)} copy-done((f32[16384]{0:T(1024)S(1)}, f32[16384]{0:T(1024)}, u32[]{:S(2)}) %copy-start.3) | copy-done | bytes 65560
  4.9 0.0 copy-start.4
  4.9 0.8 %copy-done.4 = f32[16384]{0:T(1024)S(1)} copy-done((f32[16384]{0:T(1024)S(1)}, f32[16384]{0:T(1024)}, u32[]{:S(2)}) %copy-start.4) | copy-done | bytes 65560
  5.7 0.0 copy-start.5
  5.7 0.7 %copy-done.5 = s32[4096]{0:T(1024)S(1)} copy-done((s32[4096]{0:T(1024)S(1)}, s32[4096]{0:T(1024)}, u32[]{:S(2)}) %copy-start.5) | copy-done | bytes 16408
  6.4 33.8 %exchange_fit.1 = (f32[5,128]{1,0:T(8,128)S(1)}, f32[1,16384]{1,0:T(1,128)S(1)}, f32[1,128]{1,0:T(1,128)S(1)}) custom-call(s32[1,16384]{1,0:T(1,128)S(1)} %bitcast.10, s32[1,16384]{1,0:T(1,128)S(1)} %bitcast.11, s32[32,128]{1,0:T(8,128)S(1)} %bitcast.14, s32[1,128]{1,0:T(1,128)S(1)} %bitcast.15, f32[5,16384]{1,0:T(8,128)S(1)} %copy-done, ...), custom_call_target="tpu_custom_call" | custom-call | tf_op jit(solution)/shard_map/exchange_fit/pallas_call | solution.py:264
  40.3 0.6 %copy.14 = f32[5,128]{1,0:T(8,128)} copy(f32[5,128]{1,0:T(8,128)S(1)} %get-tuple-element.12) | data formatting | bytes 5120
  40.8 0.6 %copy.15 = f32[16384]{0:T(1024)} copy(f32[16384]{0:T(1024)S(1)} %bitcast.9) | data formatting | bytes 131072
Async XLA Ops:
  0.6 0.7 %copy-start.6 = (f32[5,128]{1,0:T(8,128)S(1)}, f32[5,128]{1,0:T(8,128)}, u32[]{:S(2)}) copy-start(f32[5,128]{1,0:T(8,128)} %prior_ref.1) | copy-start | bytes 7684
  0.6 0.7 %copy-start.7 = (s32[128]{0:T(128)S(1)}, s32[128]{0:T(128)}, u32[]{:S(2)}) copy-start(s32[128]{0:T(128)} %param.11) | copy-start | bytes 1540
  1.3 1.0 %copy-start = (f32[5,16384]{1,0:T(8,128)S(1)}, f32[5,16384]{1,0:T(8,128)}, u32[]{:S(2)}) copy-start(f32[5,16384]{1,0:T(8,128)} %partials_ref.1) | copy-start | bytes 983044
  2.4 0.8 %copy-start.1 = (s32[16384]{0:T(1024)S(1)}, s32[16384]{0:T(1024)}, u32[]{:S(2)}) copy-start(s32[16384]{0:T(1024)} %param.8) | copy-start | bytes 196612
  3.2 0.8 %copy-start.2 = (s32[16384]{0:T(1024)S(1)}, s32[16384]{0:T(1024)}, u32[]{:S(2)}) copy-start(s32[16384]{0:T(1024)} %param.9) | copy-start | bytes 196612
  4.0 0.8 %copy-start.3 = (f32[16384]{0:T(1024)S(1)}, f32[16384]{0:T(1024)}, u32[]{:S(2)}) copy-start(f32[16384]{0:T(1024)} %param.13) | copy-start | bytes 196612
  4.9 0.8 %copy-start.4 = (f32[16384]{0:T(1024)S(1)}, f32[16384]{0:T(1024)}, u32[]{:S(2)}) copy-start(f32[16384]{0:T(1024)} %param.14) | copy-start | bytes 196612
  5.7 0.7 %copy-start.5 = (s32[4096]{0:T(1024)S(1)}, s32[4096]{0:T(1024)}, u32[]{:S(2)}) copy-start(s32[4096]{0:T(1024)} %param.10) | copy-start | bytes 49156

commit v2 on v1

v2 whole, which is shorter than its diff:
```python
import functools

import jax
import jax.numpy as jnp
from jax import lax
from jax.experimental import pallas as pl
from jax.experimental.pallas import tpu as pltpu
from jax.sharding import PartitionSpec as P

LANES = 128
SUBLANES = 8
UNROLL = 4
MESH = pl.DeviceIdType.MESH


def solve_rows(normal, moments):
    params = len(moments)
    factor = {}
    for column in range(params):
        running = normal[column][column]
        for earlier in range(column):
            running = running - factor[column, earlier] ** 2
        pivot_value = jnp.sqrt(running)
        factor[column, column] = pivot_value
        for target in range(column + 1, params):
            current = normal[target][column]
            for earlier in range(column):
                current = current - factor[target, earlier] * factor[column, earlier]
            factor[target, column] = current / pivot_value
    forward = []
    for target in range(params):
        current = moments[target]
        for earlier in range(target):
            current = current - factor[target, earlier] * forward[earlier]
        forward.append(current / factor[target, target])
    backward = [None] * params
    for target in reversed(range(params)):
        current = forward[target]
        for later in range(target + 1, params):
            current = current - factor[later, target] * backward[later]
        backward[target] = current / factor[target, target]
    return backward


def thirds(values):
    high = values.astype(jnp.bfloat16).astype(jnp.float32)
    rest = values - high
    middle = rest.astype(jnp.bfloat16).astype(jnp.float32)
    return [high, middle, rest - middle]


def stacked(values, rows):
    terms = thirds(values)
    spare = rows - 3 * values.shape[0]
    if spare:
        terms.append(jnp.zeros((spare, values.shape[1]), jnp.float32))
    return jnp.concatenate(terms, axis=0).astype(jnp.bfloat16)


def kernel(
    sizes,
    source_hbm, slot_hbm, owner_hbm, counts_hbm, partials_hbm, residual_hbm, weight_hbm, prior_hbm,
    updates_ref, fresh_ref, norm_ref,
    source_ref, slot_ref, owner_ref, counts_ref, partials_ref, residual_ref, weight_ref, prior_ref,
    out_buf, in_buf, hot_buf, back_out, back_in,
    load_sem, send_sem, recv_sem, back_send_sem, back_recv_sem,
):
    n, members, width, pad_slots = sizes
    params = partials_ref.shape[0]
    words = params + 2
    half = members // 2
    side = n // 2
    groups = n // members
    row_pairs = (
        (owner_hbm, owner_ref), (weight_hbm, weight_ref), (partials_hbm, partials_ref),
        (residual_hbm, residual_ref), (source_hbm, source_ref), (slot_hbm, slot_ref),
        (counts_hbm, counts_ref), (prior_hbm, prior_ref),
    )
    loads = [pltpu.make_async_copy(a, b, load_sem.at[i]) for i, (a, b) in enumerate(row_pairs)]
    for load in loads:
        load.start()
    src_local = counts_ref.shape[1]
    my_group, my_member = lax.axis_index("grp"), lax.axis_index("dev")
    me = my_group * members + my_member

    def target(i, far):
        group = (my_group + i // half) % groups
        member = (my_member // half + far) % 2 * half + (my_member % half + i % half) % half
        return group * members + member

    def origin(i, far):
        group = (my_group + groups - i // half) % groups
        member = (my_member // half + far) % 2 * half + (my_member % half + half - i % half) % half
        return group * members + member

    def coords(device):
        return (device // members, device % members)

    barrier = pltpu.get_barrier_semaphore()

    def greet(step, carry):
        peer = (me + step) % n
        pl.semaphore_signal(barrier, inc=1, device_id=coords(peer), device_id_type=MESH)
        return carry

    lax.fori_loop(1, n, greet, 0)

    loads[0].wait()
    position = me * src_local + lax.broadcasted_iota(jnp.int32, (src_local, LANES), 0)

    def invert(tile, total):
        ids = tile * LANES + lax.broadcasted_iota(jnp.int32, (1, LANES), 1)
        return total + jnp.where(owner_ref[pl.ds(tile, 1), :] == position, ids, 0)

    found = lax.fori_loop(0, owner_ref.shape[0], invert, jnp.zeros((src_local, LANES), jnp.int32))
    source_at = jnp.sum(found.astype(jnp.float32), axis=1, keepdims=True)
    for load in loads[1:]:
        load.wait()
    counts = counts_ref[...].astype(jnp.float32)
    diagonal = lax.broadcasted_iota(jnp.int32, (src_local, src_local), 0) == lax.broadcasted_iota(
        jnp.int32, (src_local, src_local), 1
    )
    count_column = jnp.sum(jnp.where(diagonal, counts, 0.0), axis=1, keepdims=True)
    first_cell = source_at * pad_slots
    end_cell = first_cell + count_column

    def prepare(step, carry):
        for part in range(UNROLL):
            k = step * UNROLL + part
            cols = pl.ds(pl.multiple_of(k * width, LANES), width)
            root = jnp.sqrt(weight_ref[:, cols])
            out_buf[k, 0:params, :] = partials_ref[:, cols] * root
            out_buf[k, params : params + 1, :] = residual_ref[:, cols] * root
            cell = source_ref[:, cols] * pad_slots + slot_ref[:, cols]
            out_buf[k, params + 1 : words, :] = cell.astype(jnp.float32)
            in_buf[k, words:SUBLANES, :] = jnp.zeros((SUBLANES - words, width), jnp.float32)
        return carry

    lax.fori_loop(0, n // UNROLL, prepare, 0)

    pl.semaphore_wait(barrier, n - 1)

    def forward(peer, slot):
        return pltpu.make_async_remote_copy(
            src_ref=out_buf.at[peer, pl.ds(0, words)],
            dst_ref=in_buf.at[slot, pl.ds(0, words)],
            send_sem=send_sem,
            recv_sem=recv_sem.at[slot],
            device_id=coords(peer),
            device_id_type=MESH,
        )

    forward(target(0, 1), me).start()

    def send(step, carry):
        forward(target(step, 1), me).start()
        forward(target(step, 0), me).start()
        return carry

    lax.fori_loop(1, side, send, 0)

    def absorb(k):
        rows = in_buf[k, 0:words, :]
        cell = rows[params + 1 : params + 2, :]
        hit = jnp.logical_and(cell >= first_cell, cell < end_cell)
        hot = jnp.where(hit, 1.0, 0.0).astype(jnp.bfloat16)
        hot_buf[k] = hot
        products = []
        for i in range(params):
            products.append(rows[i : i + 1, :] * in_buf[k])
        return lax.dot_general(
            stacked(jnp.concatenate(products, axis=0), LANES), hot, (((1,), (1,)), ((), ())),
            preferred_element_type=jnp.float32,
        )

    in_buf[me, 0:words, :] = out_buf[me, 0:words, :]
    far = origin(0, 1)
    forward(far, far).wait_recv()
    total = absorb(me) + absorb(far)

    def arrive(step, total):
        near, far = origin(step, 0), origin(step, 1)
        forward(near, near).wait_recv()
        forward(far, far).wait_recv()
        return total + absorb(near) + absorb(far)

    total = lax.fori_loop(1, side, arrive, total)

    height = params * SUBLANES
    sums = total[0:height] + total[height : 2 * height] + total[2 * height : 3 * height]
    normal = [[None] * params for _ in range(params)]
    for i in range(params):
        for j in range(i, params):
            entry = sums[i * SUBLANES + j : i * SUBLANES + j + 1]
            if i == j:
                entry = entry + prior_ref[i : i + 1, :]
            normal[i][j] = entry
            normal[j][i] = entry
    moments = [sums[i * SUBLANES + params : i * SUBLANES + params + 1] for i in range(params)]
    updates = solve_rows(normal, moments)
    for i in range(params):
        updates_ref[i : i + 1, :] = updates[i]
    blank = jnp.zeros((1, src_local), jnp.float32)
    table = jnp.concatenate(updates + [blank - 1.0] + [blank] * (SUBLANES - params - 1), axis=0)
    table = stacked(table, 4 * SUBLANES)

    def refit(step, squares):
        for part in range(UNROLL):
            k = step * UNROLL + part
            spread = jnp.dot(table, hot_buf[k], preferred_element_type=jnp.float32)
            spread = spread[0:SUBLANES] + spread[SUBLANES : 2 * SUBLANES] + spread[2 * SUBLANES : 3 * SUBLANES]
            fresh = -jnp.sum(in_buf[k] * spread, axis=0, keepdims=True)
            back_out[k, :, 0:width] = fresh
            squares = squares + fresh * fresh
        return squares

    squares = lax.fori_loop(0, n // UNROLL, refit, jnp.zeros((1, width), jnp.float32))
    lane = lax.broadcasted_iota(jnp.int32, (1, LANES), 1)
    square_sum = jnp.sum(squares, axis=1, keepdims=True)
    count_sum = jnp.sum(counts, axis=1, keepdims=True)
    tail = jnp.where(lane == 0, square_sum, jnp.where(lane == 1, count_sum, 0.0))

    def finish(k, carry):
        back_out[k, :, width : width + LANES] = tail
        return carry

    lax.fori_loop(0, n, finish, 0)
    back_in[me] = back_out[me]

    def backward(peer, slot):
        return pltpu.make_async_remote_copy(
            src_ref=back_out.at[peer],
            dst_ref=back_in.at[slot],
            send_sem=back_send_sem,
            recv_sem=back_recv_sem.at[slot],
            device_id=coords(peer),
            device_id_type=MESH,
        )

    backward(target(0, 1), me).start()

    def send_back(step, carry):
        backward(target(step, 1), me).start()
        backward(target(step, 0), me).start()
        return carry

    lax.fori_loop(1, side, send_back, 0)

    def collect(step, carry):
        peer = (me + n - step) % n
        backward(peer, peer).wait_recv()
        return carry

    lax.fori_loop(1, n, collect, 0)

    def gather_tails(k, tails):
        return tails + back_in[k, :, width : width + LANES]

    tails = lax.fori_loop(0, n, gather_tails, jnp.zeros((1, LANES), jnp.float32))
    square_total = jnp.sum(jnp.where(lane == 0, tails, 0.0), axis=1, keepdims=True)
    count_total = jnp.sum(jnp.where(lane == 1, tails, 0.0), axis=1, keepdims=True)
    norm = jnp.sqrt(square_total / count_total + 1e-06)
    norm_ref[...] = jnp.broadcast_to(norm, norm_ref.shape)
    scale = 1.0 / norm

    def emit(step, carry):
        for part in range(UNROLL):
            k = step * UNROLL + part
            cols = pl.ds(pl.multiple_of(k * width, LANES), width)
            fresh_ref[:, cols] = back_in[k, :, 0:width] * scale
        return carry

    lax.fori_loop(0, n // UNROLL, emit, 0)

    sent = (out_buf.at[pl.ds(0, n - 1), pl.ds(0, words)], back_out.at[pl.ds(0, n - 1)])
    for ref, semaphore in zip(sent, (send_sem, back_send_sem)):
        pltpu.make_async_remote_copy(
            src_ref=ref,
            dst_ref=ref,
            send_sem=semaphore,
            recv_sem=recv_sem.at[me],
            device_id=coords((me + 1) % n),
            device_id_type=MESH,
        ).wait_send()


def body(source_id, slot, owner, counts, partials, residual, weight, prior):
    members = lax.axis_size("dev")
    n = lax.axis_size("grp") * members
    params = partials.shape[0]
    row_count = residual.shape[0]
    src_local = counts.shape[0]
    block_rows = row_count // n
    width = -(-block_rows // LANES) * LANES

    def lay(array, fill):
        array = array.reshape(-1, row_count)
        if width == block_rows:
            return array
        blocks = array.reshape(-1, n, block_rows)
        blocks = jnp.pad(blocks, ((0, 0), (0, 0), (0, width - block_rows)), constant_values=fill)
        return blocks.reshape(-1, n * width)

    vmem = pl.BlockSpec(memory_space=pltpu.VMEM)
    operands = (
        lay(source_id, -1),
        lay(slot, 0),
        owner.reshape(-1, LANES),
        counts.reshape(1, src_local),
        lay(partials, 0),
        lay(residual, 0),
        lay(weight, 1),
        prior,
    )
    updates, standardized, norm = pl.pallas_call(
        functools.partial(kernel, (n, members, width, row_count // src_local)),
        out_shape=(
            jax.ShapeDtypeStruct((params, src_local), jnp.float32),
            jax.ShapeDtypeStruct((1, n * width), jnp.float32),
            jax.ShapeDtypeStruct((1, LANES), jnp.float32),
        ),
        in_specs=[pl.BlockSpec(memory_space=pltpu.HBM)] * len(operands),
        out_specs=(vmem, vmem, vmem),
        scratch_shapes=[pltpu.VMEM(operand.shape, operand.dtype) for operand in operands] + [
            pltpu.VMEM((n, SUBLANES, width), jnp.float32),
            pltpu.VMEM((n, SUBLANES, width), jnp.float32),
            pltpu.VMEM((n, src_local, width), jnp.bfloat16),
            pltpu.VMEM((n, 1, width + LANES), jnp.float32),
            pltpu.VMEM((n, 1, width + LANES), jnp.float32),
            pltpu.SemaphoreType.DMA((len(operands),)),
            pltpu.SemaphoreType.DMA,
            pltpu.SemaphoreType.DMA((n,)),
            pltpu.SemaphoreType.DMA,
            pltpu.SemaphoreType.DMA((n,)),
        ],
        compiler_params=pltpu.CompilerParams(
            collective_id=0, has_side_effects=True, vmem_limit_bytes=65000 * 1024
        ),
        name="exchange_fit",
    )(*operands)
    standardized = standardized.reshape(n, width)[:, :block_rows] if width != block_rows else standardized
    return (updates, standardized.reshape(row_count), norm[0, 0])


def solution(mesh):
    in_specs = (
        P(("grp", "dev")),
        P(("grp", "dev")),
        P(),
        P(("grp", "dev")),
        P(None, ("grp", "dev")),
        P(("grp", "dev")),
        P(("grp", "dev")),
        P(None, ("grp", "dev")),
    )
    out_specs = (P(None, ("grp", "dev")), P(("grp", "dev")), P())
    return jax.shard_map(body, mesh=mesh, in_specs=in_specs, out_specs=out_specs, check_vma=False)
```

time: 43.1 us -> 33.9 us (0.79)
  Pallas kernels: 33.8 us -> 29.1 us
  local copies, waits for them, and re-layouts: 7.02 us -> 2.74 us
    pallas_call x1, Pallas kernels: 33.8 us -> 29.1 us  [body(): pl.pallas_call(functools.partial(kernel, (n, members, width, row_count //...]
    unnamed x18 -> x6, local copies, waits for them, and re-layouts: 7.02 us -> 2.74 us
where the time goes in v2:
time: 33.9 us; the launch traced here: 33.7 us
  Pallas kernels  29.1 us (86%)
  local copies, waits for them, and re-layouts  2.74 us (8%)
  between operations  1.82 us (5%)
    pallas_call x1, Pallas kernels, body(): pl.pallas_call(functools.partial(kernel, (n, members, width, row_count //...  29.1 us
    unnamed x6, local copies, waits for them, and re-layouts  2.74 us

profile of v2, /device:TPU:0, one launch (start us, length us, event | category | flops | bytes accessed | tf_op | source)
XLA Modules:
  0.0 33.7 jit_solution(2717020394901872313)
XLA Ops:
  0.6 29.1 %exchange_fit.1 = (f32[5,128]{1,0:T(8,128)}, f32[1,16384]{1,0:T(1,128)}, f32[1,128]{1,0:T(1,128)}) custom-call(s32[1,16384]{1,0:T(1,128)} %bitcast.10, s32[1,16384]{1,0:T(1,128)} %bitcast.11, s32[32,128]{1,0:T(8,128)} %bitcast.14, s32[1,128]{1,0:T(1,128)} %bitcast.15, f32[5,16384]{1,0:T(8,128)} %partials_hbm.1, f32[1,16384]{1,0:T(1,128)} %bitcast.12, ...), custom_call_target="tpu_custom_call" | custom-call | tf_op jit(solution)/shard_map/exchange_fit/pallas_call | solution.py:315
  29.8 0.0 copy-start
  29.8 0.7 %copy-done = f32[5,128]{1,0:T(8,128)S(1)} copy-done((f32[5,128]{1,0:T(8,128)S(1)}, f32[5,128]{1,0:T(8,128)}, u32[]{:S(2)}) %copy-start) | copy-done | bytes 2584
  30.4 0.6 %copy.14 = f32[5,128]{1,0:T(8,128)} copy(f32[5,128]{1,0:T(8,128)S(1)} %copy-done) | data formatting | bytes 5120
  31.0 0.0 copy-start.1
  31.0 1.5 %copy.15 = f32[16384]{0:T(1024)} copy(f32[16384]{0:T(1024)} %bitcast.9) | data formatting | bytes 131072
  32.5 0.0 copy-done.1
Async XLA Ops:
  29.8 0.7 %copy-start = (f32[5,128]{1,0:T(8,128)S(1)}, f32[5,128]{1,0:T(8,128)}, u32[]{:S(2)}) copy-start(f32[5,128]{1,0:T(8,128)} %get-tuple-element.12) | copy-start | bytes 7684
  31.0 1.5 %copy-start.1 = (f32[1,128]{1,0:T(1,128)S(1)}, f32[1,128]{1,0:T(1,128)}, u32[]{:S(2)}) copy-start(f32[1,128]{1,0:T(1,128)} %get-tuple-element.8) | copy-start | bytes 1540

commit v3 on v2

--- a/solution.py
+++ b/solution.py
@@ -16,29 +16,29 @@
 def solve_rows(normal, moments):
     params = len(moments)
     factor = {}
+    inverse = []
     for column in range(params):
         running = normal[column][column]
         for earlier in range(column):
             running = running - factor[column, earlier] ** 2
-        pivot_value = jnp.sqrt(running)
-        factor[column, column] = pivot_value
+        inverse.append(1.0 / jnp.sqrt(running))
         for target in range(column + 1, params):
             current = normal[target][column]
             for earlier in range(column):
                 current = current - factor[target, earlier] * factor[column, earlier]
-            factor[target, column] = current / pivot_value
+            factor[target, column] = current * inverse[column]
     forward = []
     for target in range(params):
         current = moments[target]
         for earlier in range(target):
             current = current - factor[target, earlier] * forward[earlier]
-        forward.append(current / factor[target, target])
+        forward.append(current * inverse[target])
     backward = [None] * params
     for target in reversed(range(params)):
         current = forward[target]
         for later in range(target + 1, params):
             current = current - factor[later, target] * backward[later]
-        backward[target] = current / factor[target, target]
+        backward[target] = current * inverse[target]
     return backward
 
 
@@ -62,8 +62,8 @@
     source_hbm, slot_hbm, owner_hbm, counts_hbm, partials_hbm, residual_hbm, weight_hbm, prior_hbm,
     updates_ref, fresh_ref, norm_ref,
     source_ref, slot_ref, owner_ref, counts_ref, partials_ref, residual_ref, weight_ref, prior_ref,
-    out_buf, in_buf, hot_buf, back_out, back_in,
-    load_sem, send_sem, recv_sem, back_send_sem, back_recv_sem,
+    out_buf, in_buf, hot_buf, back_out, back_in, tail_out, tail_in,
+    load_sem, tail_send_sem, tail_recv_sem, send_sem, recv_sem, back_send_sem, back_recv_sem,
 ):
     n, members, width, pad_slots = sizes
     params = partials_ref.shape[0]
@@ -105,25 +105,8 @@
 
     lax.fori_loop(1, n, greet, 0)
 
-    loads[0].wait()
-    position = me * src_local + lax.broadcasted_iota(jnp.int32, (src_local, LANES), 0)
-
-    def invert(tile, total):
-        ids = tile * LANES + lax.broadcasted_iota(jnp.int32, (1, LANES), 1)
-        return total + jnp.where(owner_ref[pl.ds(tile, 1), :] == position, ids, 0)
-
-    found = lax.fori_loop(0, owner_ref.shape[0], invert, jnp.zeros((src_local, LANES), jnp.int32))
-    source_at = jnp.sum(found.astype(jnp.float32), axis=1, keepdims=True)
-    for load in loads[1:]:
+    for load in loads:
         load.wait()
-    counts = counts_ref[...].astype(jnp.float32)
-    diagonal = lax.broadcasted_iota(jnp.int32, (src_local, src_local), 0) == lax.broadcasted_iota(
-        jnp.int32, (src_local, src_local), 1
-    )
-    count_column = jnp.sum(jnp.where(diagonal, counts, 0.0), axis=1, keepdims=True)
-    first_cell = source_at * pad_slots
-    end_cell = first_cell + count_column
-
     def prepare(step, carry):
         for part in range(UNROLL):
             k = step * UNROLL + part
@@ -158,6 +141,22 @@
         return carry
 
     lax.fori_loop(1, side, send, 0)
+
+    position = me * src_local + lax.broadcasted_iota(jnp.int32, (src_local, LANES), 0)
+
+    def invert(tile, total):
+        ids = tile * LANES + lax.broadcasted_iota(jnp.int32, (1, LANES), 1)
+        return total + jnp.where(owner_ref[pl.ds(tile, 1), :] == position, ids, 0)
+
+    found = lax.fori_loop(0, owner_ref.shape[0], invert, jnp.zeros((src_local, LANES), jnp.int32))
+    source_at = jnp.sum(found.astype(jnp.float32), axis=1, keepdims=True)
+    counts = counts_ref[...].astype(jnp.float32)
+    diagonal = lax.broadcasted_iota(jnp.int32, (src_local, src_local), 0) == lax.broadcasted_iota(
+        jnp.int32, (src_local, src_local), 1
+    )
+    count_column = jnp.sum(jnp.where(diagonal, counts, 0.0), axis=1, keepdims=True)
+    first_cell = source_at * pad_slots
+    end_cell = first_cell + count_column
 
     def absorb(k):
         rows = in_buf[k, 0:words, :]
@@ -204,29 +203,6 @@
     table = jnp.concatenate(updates + [blank - 1.0] + [blank] * (SUBLANES - params - 1), axis=0)
     table = stacked(table, 4 * SUBLANES)
 
-    def refit(step, squares):
-        for part in range(UNROLL):
-            k = step * UNROLL + part
-            spread = jnp.dot(table, hot_buf[k], preferred_element_type=jnp.float32)
-            spread = spread[0:SUBLANES] + spread[SUBLANES : 2 * SUBLANES] + spread[2 * SUBLANES : 3 * SUBLANES]
-            fresh = -jnp.sum(in_buf[k] * spread, axis=0, keepdims=True)
-            back_out[k, :, 0:width] = fresh
-            squares = squares + fresh * fresh
-        return squares
-
-    squares = lax.fori_loop(0, n // UNROLL, refit, jnp.zeros((1, width), jnp.float32))
-    lane = lax.broadcasted_iota(jnp.int32, (1, LANES), 1)
-    square_sum = jnp.sum(squares, axis=1, keepdims=True)
-    count_sum = jnp.sum(counts, axis=1, keepdims=True)
-    tail = jnp.where(lane == 0, square_sum, jnp.where(lane == 1, count_sum, 0.0))
-
-    def finish(k, carry):
-        back_out[k, :, width : width + LANES] = tail
-        return carry
-
-    lax.fori_loop(0, n, finish, 0)
-    back_in[me] = back_out[me]
-
     def backward(peer, slot):
         return pltpu.make_async_remote_copy(
             src_ref=back_out.at[peer],
@@ -237,24 +213,67 @@
             device_id_type=MESH,
         )
 
-    backward(target(0, 1), me).start()
-
-    def send_back(step, carry):
-        backward(target(step, 1), me).start()
+    def summary(peer, slot):
+        return pltpu.make_async_remote_copy(
+            src_ref=tail_out,
+            dst_ref=tail_in.at[slot],
+            send_sem=tail_send_sem,
+            recv_sem=tail_recv_sem.at[slot],
+            device_id=coords(peer),
+            device_id_type=MESH,
+        )
+
+    def refit(k):
+        spread = jnp.dot(table, hot_buf[k], preferred_element_type=jnp.float32)
+        spread = spread[0:SUBLANES] + spread[SUBLANES : 2 * SUBLANES] + spread[2 * SUBLANES : 3 * SUBLANES]
+        fresh = -jnp.sum(in_buf[k] * spread, axis=0, keepdims=True)
+        back_out[k] = fresh
+        return fresh * fresh
+
+    def refit_far(step, squares):
+        for part in range(UNROLL):
+            squares = squares + refit(target(step * UNROLL + part, 1))
+        for part in range(UNROLL):
+            peer = target(step * UNROLL + part, 1)
+            backward(peer, me).start()
+        return squares
+
+    def refit_near(step, squares):
+        for part in range(UNROLL):
+            squares = squares + refit(target(step * UNROLL + part, 0))
+        return squares
+
+    squares = lax.fori_loop(0, side // UNROLL, refit_far, jnp.zeros((1, width), jnp.float32))
+    squares = lax.fori_loop(0, side // UNROLL, refit_near, squares)
+    lane = lax.broadcasted_iota(jnp.int32, (1, LANES), 1)
+    square_sum = jnp.sum(squares, axis=1, keepdims=True)
+    count_sum = jnp.sum(counts, axis=1, keepdims=True)
+    tail_out[...] = jnp.where(lane == 0, square_sum, jnp.where(lane == 1, count_sum, 0.0))
+
+    def send_far_tail(step, carry):
+        summary(target(step, 1), me).start()
+        return carry
+
+    def send_near(step, carry):
         backward(target(step, 0), me).start()
-        return carry
-
-    lax.fori_loop(1, side, send_back, 0)
+        summary(target(step, 0), me).start()
+        return carry
+
+    lax.fori_loop(0, side, send_far_tail, 0)
+    lax.fori_loop(1, side, send_near, 0)
+    back_in[me] = back_out[me]
+    tail_in[me] = tail_out[...]
 
     def collect(step, carry):
         peer = (me + n - step) % n
         backward(peer, peer).wait_recv()
+        summary(peer, peer).wait_recv()
         return carry
 
     lax.fori_loop(1, n, collect, 0)
 
     def gather_tails(k, tails):
-        return tails + back_in[k, :, width : width + LANES]
+        return tails + tail_in[k]
 
     tails = lax.fori_loop(0, n, gather_tails, jnp.zeros((1, LANES), jnp.float32))
     square_total = jnp.sum(jnp.where(lane == 0, tails, 0.0), axis=1, keepdims=True)
@@ -267,13 +286,13 @@
         for part in range(UNROLL):
             k = step * UNROLL + part
             cols = pl.ds(pl.multiple_of(k * width, LANES), width)
-            fresh_ref[:, cols] = back_in[k, :, 0:width] * scale
+            fresh_ref[:, cols] = back_in[k] * scale
         return carry
 
     lax.fori_loop(0, n // UNROLL, emit, 0)
 
-    sent = (out_buf.at[pl.ds(0, n - 1), pl.ds(0, words)], back_out.at[pl.ds(0, n - 1)])
-    for ref, semaphore in zip(sent, (send_sem, back_send_sem)):
+    sent = (out_buf.at[pl.ds(0, n - 1), pl.ds(0, words)], back_out.at[pl.ds(0, n - 1)], tail_in.at[pl.ds(0, n - 1)])
+    for ref, semaphore in zip(sent, (send_sem, back_send_sem, tail_send_sem)):
         pltpu.make_async_remote_copy(
             src_ref=ref,
             dst_ref=ref,
@@ -282,6 +301,15 @@
             device_id=coords((me + 1) % n),
             device_id_type=MESH,
         ).wait_send()
+
+
+def release(a_ref, b_ref, c_ref, a_out, b_out, c_out, sem):
+    pairs = ((a_ref, a_out), (b_ref, b_out), (c_ref, c_out))
+    copies = [pltpu.make_async_copy(x, y, sem.at[i]) for i, (x, y) in enumerate(pairs)]
+    for copy in copies:
+        copy.start()
+    for copy in copies:
+        copy.wait()
 
 
 def body(source_id, slot, owner, counts, partials, residual, weight, prior):
@@ -325,9 +353,13 @@
             pltpu.VMEM((n, SUBLANES, width), jnp.float32),
             pltpu.VMEM((n, SUBLANES, width), jnp.float32),
             pltpu.VMEM((n, src_local, width), jnp.bfloat16),
-            pltpu.VMEM((n, 1, width + LANES), jnp.float32),
-            pltpu.VMEM((n, 1, width + LANES), jnp.float32),
+            pltpu.VMEM((n, 1, width), jnp.float32),
+            pltpu.VMEM((n, 1, width), jnp.float32),
+            pltpu.VMEM((1, LANES), jnp.float32),
+            pltpu.VMEM((n, 1, LANES), jnp.float32),
             pltpu.SemaphoreType.DMA((len(operands),)),
+            pltpu.SemaphoreType.DMA,
+            pltpu.SemaphoreType.DMA((n,)),
             pltpu.SemaphoreType.DMA,
             pltpu.SemaphoreType.DMA((n,)),
             pltpu.SemaphoreType.DMA,
@@ -338,6 +370,15 @@
         ),
         name="exchange_fit",
     )(*operands)
+    results = (updates, standardized, norm)
+    updates, standardized, norm = pl.pallas_call(
+        release,
+        out_shape=tuple(jax.ShapeDtypeStruct(r.shape, r.dtype) for r in results),
+        in_specs=[vmem] * 3,
+        out_specs=[pl.BlockSpec(memory_space=pltpu.HBM)] * 3,
+        scratch_shapes=[pltpu.SemaphoreType.DMA((3,))],
+        name="release",
+    )(*results)
     standardized = standardized.reshape(n, width)[:, :block_rows] if width != block_rows else standardized
     return (updates, standardized.reshape(row_count), norm[0, 0])
 

time: 33.9 us -> 31.8 us (0.938)
  local copies, waits for them, and re-layouts: 2.74 us -> 0 us
  Pallas kernels: 29.1 us -> 31 us
  between operations: 1.82 us -> 0.64 us
    unnamed x6 -> x0, local copies, waits for them, and re-layouts: 2.74 us -> none
    pallas_call x0 -> x1, Pallas kernels: none -> 1.5 us  [body(): pl.pallas_call(release, out_shape=tuple((jax.ShapeDtypeStruct(r.shape, r....]
    pallas_call x1, Pallas kernels: 29.1 us -> 29.5 us  [body(): pl.pallas_call(functools.partial(kernel, (n, members, width, row_count //...]
where the time goes in v3:
time: 31.8 us; the launch traced here: 31.6 us
  Pallas kernels  31 us (97%)
  between operations  0.64 us (2%)
    pallas_call x1, Pallas kernels, body(): pl.pallas_call(functools.partial(kernel, (n, members, width, row_count //...  29.5 us
    pallas_call x1, Pallas kernels, body(): pl.pallas_call(release, out_shape=tuple((jax.ShapeDtypeStruct(r.shape, r....  1.5 us

profile of v3, /device:TPU:0, one launch (start us, length us, event | category | flops | bytes accessed | tf_op | source)
XLA Modules:
  0.0 31.6 jit_solution(15044053900510560312)
XLA Ops:
  0.6 29.5 %exchange_fit.1 = (f32[5,128]{1,0:T(8,128)}, f32[1,16384]{1,0:T(1,128)}, f32[1,128]{1,0:T(1,128)}) custom-call(s32[1,16384]{1,0:T(1,128)} %bitcast.9, s32[1,16384]{1,0:T(1,128)} %bitcast.10, s32[32,128]{1,0:T(8,128)} %bitcast.13, s32[1,128]{1,0:T(1,128)} %bitcast.14, f32[5,16384]{1,0:T(8,128)} %partials_hbm.1, f32[1,16384]{1,0:T(1,128)} %bitcast.11, ...), custom_call_target="tpu_custom_call" | custom-call | tf_op jit(solution)/shard_map/exchange_fit/pallas_call | solution.py:343
  30.1 1.5 %release.1 = (f32[5,128]{1,0:T(8,128)}, f32[1,16384]{1,0:T(1,128)}, f32[1,128]{1,0:T(1,128)}) custom-call(f32[5,128]{1,0:T(8,128)} %get-tuple-element.9.a_ref, f32[1,16384]{1,0:T(1,128)} %get-tuple-element.10.b_ref, f32[1,128]{1,0:T(1,128)} %get-tuple-element.11.c_ref), custom_call_target="tpu_custom_call" | custom-call | tf_op jit(solution)/shard_map/release/pallas_call | solution.py:374

commit v4 on v3

--- a/solution.py
+++ b/solution.py
@@ -208,7 +208,7 @@
             src_ref=back_out.at[peer],
             dst_ref=back_in.at[slot],
             send_sem=back_send_sem,
-            recv_sem=back_recv_sem.at[slot],
+            recv_sem=back_recv_sem,
             device_id=coords(peer),
             device_id_type=MESH,
         )
@@ -218,7 +218,7 @@
             src_ref=tail_out,
             dst_ref=tail_in.at[slot],
             send_sem=tail_send_sem,
-            recv_sem=tail_recv_sem.at[slot],
+            recv_sem=tail_recv_sem,
             device_id=coords(peer),
             device_id_type=MESH,
         )
@@ -227,15 +227,12 @@
         spread = jnp.dot(table, hot_buf[k], preferred_element_type=jnp.float32)
         spread = spread[0:SUBLANES] + spread[SUBLANES : 2 * SUBLANES] + spread[2 * SUBLANES : 3 * SUBLANES]
         fresh = -jnp.sum(in_buf[k] * spread, axis=0, keepdims=True)
-        back_out[k] = fresh
+        back_out[k, :, 0:width] = fresh
         return fresh * fresh
 
     def refit_far(step, squares):
         for part in range(UNROLL):
             squares = squares + refit(target(step * UNROLL + part, 1))
-        for part in range(UNROLL):
-            peer = target(step * UNROLL + part, 1)
-            backward(peer, me).start()
         return squares
 
     def refit_near(step, squares):
@@ -250,30 +247,38 @@
     count_sum = jnp.sum(counts, axis=1, keepdims=True)
     tail_out[...] = jnp.where(lane == 0, square_sum, jnp.where(lane == 1, count_sum, 0.0))
 
+    def finish(step, carry):
+        for part in range(UNROLL):
+            back_out[step * UNROLL + part, :, width : width + LANES] = tail_out[...]
+        return carry
+
+    lax.fori_loop(0, n // UNROLL, finish, 0)
+
     def send_far_tail(step, carry):
-        summary(target(step, 1), me).start()
+        backward(target(step, 1), me).start()
         return carry
 
     def send_near(step, carry):
         backward(target(step, 0), me).start()
-        summary(target(step, 0), me).start()
         return carry
 
     lax.fori_loop(0, side, send_far_tail, 0)
     lax.fori_loop(1, side, send_near, 0)
     back_in[me] = back_out[me]
-    tail_in[me] = tail_out[...]
-
-    def collect(step, carry):
-        peer = (me + n - step) % n
-        backward(peer, peer).wait_recv()
-        summary(peer, peer).wait_recv()
-        return carry
-
-    lax.fori_loop(1, n, collect, 0)
+
+    others = pl.ds(0, n - 1)
+    for ref, semaphore in ((back_in.at[others], back_recv_sem),):
+        pltpu.make_async_remote_copy(
+            src_ref=ref,
+            dst_ref=ref,
+            send_sem=back_send_sem,
+            recv_sem=semaphore,
+            device_id=coords((me + 1) % n),
+            device_id_type=MESH,
+        ).wait_recv()
 
     def gather_tails(k, tails):
-        return tails + tail_in[k]
+        return tails + back_in[k, :, width : width + LANES]
 
     tails = lax.fori_loop(0, n, gather_tails, jnp.zeros((1, LANES), jnp.float32))
     square_total = jnp.sum(jnp.where(lane == 0, tails, 0.0), axis=1, keepdims=True)
@@ -286,13 +291,13 @@
         for part in range(UNROLL):
             k = step * UNROLL + part
             cols = pl.ds(pl.multiple_of(k * width, LANES), width)
-            fresh_ref[:, cols] = back_in[k] * scale
+            fresh_ref[:, cols] = back_in[k, :, 0:width] * scale
         return carry
 
     lax.fori_loop(0, n // UNROLL, emit, 0)
 
-    sent = (out_buf.at[pl.ds(0, n - 1), pl.ds(0, words)], back_out.at[pl.ds(0, n - 1)], tail_in.at[pl.ds(0, n - 1)])
-    for ref, semaphore in zip(sent, (send_sem, back_send_sem, tail_send_sem)):
+    sent = (out_buf.at[pl.ds(0, n - 1), pl.ds(0, words)], back_out.at[pl.ds(0, n - 1)])
+    for ref, semaphore in zip(sent, (send_sem, back_send_sem)):
         pltpu.make_async_remote_copy(
             src_ref=ref,
             dst_ref=ref,
@@ -353,17 +358,17 @@
             pltpu.VMEM((n, SUBLANES, width), jnp.float32),
             pltpu.VMEM((n, SUBLANES, width), jnp.float32),
             pltpu.VMEM((n, src_local, width), jnp.bfloat16),
-            pltpu.VMEM((n, 1, width), jnp.float32),
-            pltpu.VMEM((n, 1, width), jnp.float32),
+            pltpu.VMEM((n, 1, width + LANES), jnp.float32),
+            pltpu.VMEM((n, 1, width + LANES), jnp.float32),
             pltpu.VMEM((1, LANES), jnp.float32),
             pltpu.VMEM((n, 1, LANES), jnp.float32),
             pltpu.SemaphoreType.DMA((len(operands),)),
             pltpu.SemaphoreType.DMA,
-            pltpu.SemaphoreType.DMA((n,)),
+            pltpu.SemaphoreType.DMA,
             pltpu.SemaphoreType.DMA,
             pltpu.SemaphoreType.DMA((n,)),
             pltpu.SemaphoreType.DMA,
-            pltpu.SemaphoreType.DMA((n,)),
+            pltpu.SemaphoreType.DMA,
         ],
         compiler_params=pltpu.CompilerParams(
             collective_id=0, has_side_effects=True, vmem_limit_bytes=65000 * 1024

time: 31.8 us -> 30.9 us (0.972)
  Pallas kernels: 31 us -> 30 us
    pallas_call x1, Pallas kernels: 29.5 us -> 28.5 us  [body(): pl.pallas_call(functools.partial(kernel, (n, members, width, row_count //...]
where the time goes in v4:
time: 30.9 us; the launch traced here: 30.7 us
  Pallas kernels  30 us (97%)
  between operations  0.64 us (2%)
    pallas_call x1, Pallas kernels, body(): pl.pallas_call(functools.partial(kernel, (n, members, width, row_count //...  28.5 us
    pallas_call x1, Pallas kernels, body(): pl.pallas_call(release, out_shape=tuple((jax.ShapeDtypeStruct(r.shape, r....  1.5 us

profile of v4, /device:TPU:0, one launch (start us, length us, event | category | flops | bytes accessed | tf_op | source)
XLA Modules:
  0.0 30.7 jit_solution(6889202244856008317)
XLA Ops:
  0.6 28.5 %exchange_fit.1 = (f32[5,128]{1,0:T(8,128)}, f32[1,16384]{1,0:T(1,128)}, f32[1,128]{1,0:T(1,128)}) custom-call(s32[1,16384]{1,0:T(1,128)} %bitcast.9, s32[1,16384]{1,0:T(1,128)} %bitcast.10, s32[32,128]{1,0:T(8,128)} %bitcast.13, s32[1,128]{1,0:T(1,128)} %bitcast.14, f32[5,16384]{1,0:T(8,128)} %partials_hbm.1, f32[1,16384]{1,0:T(1,128)} %bitcast.11, ...), custom_call_target="tpu_custom_call" | custom-call | tf_op jit(solution)/shard_map/exchange_fit/pallas_call | solution.py:348
  29.1 1.5 %release.1 = (f32[5,128]{1,0:T(8,128)}, f32[1,16384]{1,0:T(1,128)}, f32[1,128]{1,0:T(1,128)}) custom-call(f32[5,128]{1,0:T(8,128)} %get-tuple-element.9.a_ref, f32[1,16384]{1,0:T(1,128)} %get-tuple-element.10.b_ref, f32[1,128]{1,0:T(1,128)} %get-tuple-element.11.c_ref), custom_call_target="tpu_custom_call" | custom-call | tf_op jit(solution)/shard_map/release/pallas_call | solution.py:379
